TPU v7x, 32 devices: a whole 2x2x4 slice. The times are simulated.
32 devices in a mesh: mp: 8 (over z, y), rows: 4 (over x, core).
Axes of the slice: x: 2, y: 2, z: 4, core: 2. Of those that a mesh axis runs over, the one named last changes fastest.
Arguments:
- inputs: float32 [1024, 16384], P('rows', 'mp'), may hold values from -6 to 6
- weight: float32 [512, 16384], P('mp'), may hold values from -1.5 to 1.5, as said below
Outputs:
- row_scale: float32 [1024], P('rows')
- product: float32 [512, 1024], P('mp', 'rows')
- normalized: float32 [512, 1024], P('mp')
Inputs may be any that keep to these rules, and one draw needn't show every extreme that they name: A weight matrix whose rows carry different scales.
All inputs are finite; a program needn't handle non-finite values. Where the computation divides by a largest or mean magnitude, that divisor is 1e-20 or more.
Results may differ from a plain program's by a relative error of at most 0.0003.
Values may be sent and summed in bfloat16 or wider, within the bound.
A program may use at most 64 MiB of HBM per device.

v0:
```python
import jax
import jax.numpy as jnp
from jax import lax
from jax.sharding import PartitionSpec as P

epsilon = 1e-06


def split_two(values):
    scaled = values * 128.0
    first = jnp.floor(scaled)
    second = jnp.floor((scaled - first) * 256.0)
    return (first.astype(jnp.bfloat16), second.astype(jnp.bfloat16))


def matmul(w_side, x_side):
    return lax.dot_general(
        w_side, x_side, (((1,), (1,)), ((), ())), preferred_element_type=jnp.float32
    )


def pair_sums(x_parts, w_parts):
    level_zero = matmul(w_parts[0], x_parts[0])
    level_one = matmul(w_parts[0], x_parts[1]) + matmul(w_parts[1], x_parts[0])
    return (level_zero, level_one)


def combine_levels(levels):
    return levels[0] + levels[1] / 256.0


def per_device(inputs, weight):
    col_scale = jnp.max(jnp.abs(weight), axis=1) + epsilon
    w_parts = split_two(weight / col_scale[:, None])
    row_scale = lax.pmax(jnp.max(jnp.abs(inputs), axis=1), "mp") + epsilon
    x_parts = split_two(inputs / row_scale[:, None])
    stacked = jnp.stack(w_parts, axis=0)
    moved = lax.all_to_all(stacked, "mp", split_axis=2, concat_axis=1, tiled=True)
    partial_term = combine_levels(pair_sums(x_parts, (moved[0], moved[1])))
    combined = lax.psum_scatter(partial_term, "mp", scatter_dimension=0, tiled=True)
    product = combined * col_scale[:, None] * row_scale[None, :] / 16384.0
    squares = lax.psum(jnp.sum(product * product, axis=0), "mp")
    mean_square = squares / (weight.shape[0] * lax.axis_size("mp"))
    normalized = product * lax.rsqrt(mean_square + epsilon)[None, :]
    gathered_rows = lax.all_gather(normalized, "rows", axis=1, tiled=True)
    return (row_scale, product, gathered_rows)


def solution(mesh):
    return jax.shard_map(
        per_device,
        mesh=mesh,
        in_specs=(P("rows", "mp"), P("mp", None)),
        out_specs=(P("rows"), P("mp", "rows"), P("mp", None)),
        check_vma=False,
    )
```

profile of v0, /device:TPU:0, one launch (start us, length us, event | category | flops | bytes accessed | tf_op | source)
XLA Modules:
  0.0 281.4 jit_solution(13112939245431465066)
XLA Ops:
  7.2 0.0 copy-start
  7.2 2.6 abs_reduce_fusion
  9.8 0.8 copy-done
  10.6 1.1 fusion.7
  11.7 2.3 pad_maximum_fusion
  14.0 17.8 %copy.12 = bf16[2,64,16384]{1,0,2:T(2,128)(2,1)} copy(bf16[2,64,16384]{2,1,0:T(8,128)(2,1)} %pad_maximum_fusion) | data formatting | bytes 8388608 | tf_op jit(solution)/shard_map/stack | solution.py:37
  31.8 10.5 %reshape.16 = bf16[8,2,131072]{2,1,0:T(2,128)(2,1)} reshape(bf16[16384,2,64]{2,1,0:T(2,128)(2,1)} %bitcast.13) | data formatting | bytes 8388608
  42.3 0.0 copy-start.1
  42.3 7.4 %all-to-all-start = ((bf16[8,2,131072]{2,1,0:T(2,128)(2,1)}), bf16[8,2,131072]{2,1,0:T(2,128)(2,1)}, u32[]{:S(2)}, u32[]{:S(2)}) async-start(bf16[8,2,131072]{2,1,0:T(2,128)(2,1)} %reshape.16), calls=%async_computation | async-start | bytes 8388608 | tf_op jit(solution)/shard_map/all_to_all | solution.py:38
  49.7 0.0 reduce-scatter.2.cloned.1.call-start
  49.8 0.0 copy-done.1
  49.8 0.2 abs_reduce_fusion.1
  50.0 85.0 %pmax.7 = f32[256]{0:T(256)S(1)} all-reduce(f32[256]{0:T(256)S(1)} %abs_reduce_fusion.1), channel_id=1, replica_groups=mesh['mp'=8,'rows'=4] {'mp'}, use_global_device_ids=true, to_apply=%region_1.0 | all-reduce | flops 256 | bytes 2048 | tf_op jit(solution)/shard_map/pmax | solution.py:35
  135.0 0.0 copy-start.2
  135.0 8.1 %all-to-all-done = bf16[8,2,131072]{2,1,0:T(2,128)(2,1)} async-done(((bf16[8,2,131072]{2,1,0:T(2,128)(2,1)}), bf16[8,2,131072]{2,1,0:T(2,128)(2,1)}, u32[]{:S(2)}, u32[]{:S(2)}) %all-to-all-start) | async-done | bytes 4194336 | tf_op jit(solution)/shard_map/all_to_all | solution.py:38
  143.1 10.3 %reshape.17 = bf16[16384,2,64]{2,1,0:T(2,128)(2,1)} reshape(bf16[8,2,131072]{2,1,0:T(2,128)(2,1)} %all-to-all-done) | data formatting | bytes 8388608
  153.4 13.6 %copy.16 = bf16[2,64,8,2048]{3,2,1,0:T(8,128)(2,1)} copy(bf16[2,64,8,2048]{1,0,3,2:T(2,128)(2,1)} %bitcast.14) | data formatting | bytes 8388608 | tf_op jit(solution)/shard_map/all_to_all | solution.py:38
  167.0 2.7 fusion.16
  169.7 1.2 copy.14
  170.9 1.2 copy.15
  172.1 1.0 fusion.9
  173.1 0.9 fusion.8
  174.0 1.7 convolution_add_fusion.1
  175.6 0.0 reduce-scatter.2.cloned.1.call-update
  175.6 70.5 %reduce-scatter.2.cloned.1.call-done = f32[64,256]{1,0:T(8,128)} async-done(((f32[512,256]{1,0:T(8,128)}), f32[64,256]{1,0:T(8,128)}) %reduce-scatter.2.cloned.1.call-update) | async-done | bytes 65552 | tf_op jit(solution)/shard_map/reduce_scatter | solution.py:40
  246.1 1.6 multiply_reduce_fusion
  247.7 19.4 %psum.7 = f32[256]{0:T(256)S(1)} all-reduce(f32[256]{0:T(256)S(1)} %get-tuple-element.3), channel_id=1, replica_groups=mesh['mp'=8,'rows'=4] {'mp'}, use_global_device_ids=true, to_apply=%region_5.0 | all-reduce | flops 256 | bytes 2048 | tf_op jit(solution)/shard_map/psum | solution.py:42
  267.1 0.0 copy-done.2
  267.1 0.9 fusion.12
  268.0 5.8 %all_gather.3 = f32[64,1024]{1,0:T(8,128)S(1)} all-gather(f32[64,256]{1,0:T(8,128)S(1)} %fusion.12), channel_id=1, replica_groups=mesh['mp'=8,'rows'=4] {'rows'}, dimensions={1}, use_global_device_ids=true | all-gather | bytes 327680 | tf_op jit(solution)/shard_map/all_gather | solution.py:45
  273.8 0.7 copy.18
  (3 shorter events, 0.0 us)
Async XLA Ops:
  7.2 3.5 %copy-start = (f32[64,16384]{1,0:T(8,128)S(1)}, f32[64,16384]{1,0:T(8,128)}, u32[]{:S(2)}) copy-start(f32[64,16384]{1,0:T(8,128)} %param.3) | copy-start | bytes 12582916
  42.3 7.5 %copy-start.1 = (f32[256,2048]{1,0:T(8,128)S(1)}, f32[256,2048]{1,0:T(8,128)}, u32[]{:S(2)}) copy-start(f32[256,2048]{1,0:T(8,128)} %param.2) | copy-start | bytes 6291460
  42.3 100.8 %all-to-all-start = ((bf16[8,2,131072]{2,1,0:T(2,128)(2,1)}), bf16[8,2,131072]{2,1,0:T(2,128)(2,1)}, u32[]{:S(2)}, u32[]{:S(2)}) async-start(bf16[8,2,131072]{2,1,0:T(2,128)(2,1)} %reshape.16), calls=%async_computation | async-start | bytes 8388608 | tf_op jit(solution)/shard_map/all_to_all | solution.py:38
  49.7 196.4 %reduce-scatter.2.cloned.1.call-start = ((), (), s32[]{:S(2)}) async-start(), calls=%async_computation.2 | async-start | bytes 589824 | tf_op jit(solution)/shard_map/reduce_scatter | solution.py:40
  135.0 132.1 %copy-start.2 = (f32[256]{0:T(256)}, f32[256]{0:T(256)S(1)}, u32[]{:S(2)}) copy-start(f32[256]{0:T(256)S(1)} %broadcast_add_fusion) | copy-start | bytes 3076
Sparse Core Ops, SparseCore 0:
  175.8 70.3 reduce-scatter.1
where the time goes:
time: 283 us; the launch traced here: 281 us
  blocking collectives  110 us (39%)
  waiting for transfers between devices  78.6 us (28%)
  local copies, waits for them, and re-layouts  58.7 us (21%)
  between operations  14.1 us (5%)
  other arithmetic  8.76 us (3%)
  starting transfers between devices  7.48 us (3%)
  matrix products  3.54 us (1%)
    pmax x1, blocking collectives, per_device(): row_scale = lax.pmax(jnp.max(jnp.abs(inputs), axis=1), 'mp') + epsilon  85 us
    reduce_scatter x1, waiting for transfers between devices, per_device(): lax.psum_scatter(partial_term, 'mp', scatter_dimension=0, tiled=True)  70.5 us
    unnamed x9, local copies, waits for them, and re-layouts  22.3 us
    psum x1, blocking collectives, per_device(): squares = lax.psum(jnp.sum(product * product, axis=0), 'mp')  19.4 us
    another operation x1, local copies, waits for them, and re-layouts, per_device(): stacked = jnp.stack(w_parts, axis=0)  17.8 us
    all_to_all x1, local copies, waits for them, and re-layouts, per_device(): lax.all_to_all(stacked, 'mp', split_axis=2, concat_axis=1, tiled=True)  13.6 us
    all_to_all x1, waiting for transfers between devices, per_device(): lax.all_to_all(stacked, 'mp', split_axis=2, concat_axis=1, tiled=True)  8.12 us
    all_to_all x1, starting transfers between devices, per_device(): lax.all_to_all(stacked, 'mp', split_axis=2, concat_axis=1, tiled=True)  7.44 us
  transfers between devices with their start and end apart: 2, of which 2 were waited for; matrix products, arithmetic and copies ran while one was open for 0% of the time, Pallas kernels for 0%

commit v1 on v0

--- a/solution.py
+++ b/solution.py
@@ -35,7 +35,9 @@
     row_scale = lax.pmax(jnp.max(jnp.abs(inputs), axis=1), "mp") + epsilon
     x_parts = split_two(inputs / row_scale[:, None])
     stacked = jnp.stack(w_parts, axis=0)
-    moved = lax.all_to_all(stacked, "mp", split_axis=2, concat_axis=1, tiled=True)
+    shards = jnp.split(stacked, lax.axis_size("mp"), axis=2)
+    got = lax.all_to_all(jnp.stack(shards), "mp", 0, 0)
+    moved = jnp.concatenate(got, axis=1)
     partial_term = combine_levels(pair_sums(x_parts, (moved[0], moved[1])))
     combined = lax.psum_scatter(partial_term, "mp", scatter_dimension=0, tiled=True)
     product = combined * col_scale[:, None] * row_scale[None, :] / 16384.0

time: 283 us -> 232 us (0.82)
  local copies, waits for them, and re-layouts: 58.7 us -> 4.22 us
  other arithmetic: 8.76 us -> 13.2 us
    unnamed x9 -> x7, local copies, waits for them, and re-layouts: 22.3 us -> 1.49 us
    another operation x1 -> x0, local copies, waits for them, and re-layouts: 17.8 us -> none  [per_device(): stacked = jnp.stack(w_parts, axis=0)]
    all_to_all x1 -> x0, local copies, waits for them, and re-layouts: 13.6 us -> none  [per_device(): lax.all_to_all(stacked, 'mp', split_axis=2, concat_axis=1, tiled=True)]
    unnamed x0 -> x7, other arithmetic: none -> 5.97 us
where the time goes in v1:
time: 232 us; the launch traced here: 231 us
  blocking collectives  110 us (47%)
  waiting for transfers between devices  78.7 us (34%)
  between operations  14.1 us (6%)
  other arithmetic  13.2 us (6%)
  starting transfers between devices  7.48 us (3%)
  local copies, waits for them, and re-layouts  4.22 us (2%)
  matrix products  3.51 us (2%)
    pmax x1, blocking collectives, per_device(): row_scale = lax.pmax(jnp.max(jnp.abs(inputs), axis=1), 'mp') + epsilon  85 us
    reduce_scatter x1, waiting for transfers between devices, per_device(): lax.psum_scatter(partial_term, 'mp', scatter_dimension=0, tiled=True)  70.6 us
    psum x1, blocking collectives, per_device(): squares = lax.psum(jnp.sum(product * product, axis=0), 'mp')  19.3 us
    all_to_all x1, waiting for transfers between devices, per_device(): got = lax.all_to_all(jnp.stack(shards), 'mp', 0, 0)  8.12 us
    all_to_all x1, starting transfers between devices, per_device(): got = lax.all_to_all(jnp.stack(shards), 'mp', 0, 0)  7.44 us
    unnamed x7, other arithmetic  5.97 us
    all_gather x1, blocking collectives, per_device(): gathered_rows = lax.all_gather(normalized, 'rows', axis=1, tiled=True)  5.78 us
  transfers between devices with their start and end apart: 2, of which 2 were waited for; matrix products, arithmetic and copies ran while one was open for 0% of the time, Pallas kernels for 0%

profile of v1, /device:TPU:0, one launch (start us, length us, event | category | flops | bytes accessed | tf_op | source)
XLA Modules:
  0.0 231.3 jit_solution(3200941102287751130)
XLA Ops:
  7.2 0.0 copy-start
  7.2 2.6 %abs_reduce_fusion = f32[64]{0:T(128)S(1)} fusion(f32[64,16384]{1,0:T(8,128)} %param.3), kind=kLoop, calls=%fused_computation.20 | loop fusion | flops 2097088 | bytes 4194560 | tf_op jit(solution)/shard_map/reduce_max | solution.py:33
  9.8 0.8 copy-done
  10.6 1.1 fusion.7
  11.7 0.8 bitcast_dynamic-update-slice_fusion.6
  12.5 0.9 bitcast_dynamic-update-slice_fusion.5
  13.4 0.9 bitcast_dynamic-update-slice_fusion.4
  14.2 0.9 bitcast_dynamic-update-slice_fusion.3
  15.1 0.9 bitcast_dynamic-update-slice_fusion.2
  16.0 0.9 bitcast_dynamic-update-slice_fusion.1
  16.8 0.8 bitcast_dynamic-update-slice_fusion
  17.7 0.9 fusion.20
  18.5 0.0 copy-start.1
  18.5 7.4 %all-to-all-start = ((bf16[8,2,64,2048]{3,2,1,0:T(8,128)(2,1)}), bf16[8,2,64,2048]{3,2,1,0:T(8,128)(2,1)}, u32[]{:S(2)}, u32[]{:S(2)}) async-start(bf16[8,2,64,2048]{3,2,1,0:T(8,128)(2,1)} %fusion.20), calls=%async_computation | async-start | bytes 8388608 | tf_op jit(solution)/shard_map/all_to_all | solution.py:39
  26.0 0.0 reduce-scatter.2.cloned.1.call-start
  26.0 0.0 copy-done.1
  26.0 0.2 abs_reduce_fusion.1
  26.2 85.0 %pmax.7 = f32[256]{0:T(256)S(1)} all-reduce(f32[256]{0:T(256)S(1)} %abs_reduce_fusion.1), channel_id=1, replica_groups=mesh['mp'=8,'rows'=4] {'mp'}, use_global_device_ids=true, to_apply=%region_1.0 | all-reduce | flops 256 | bytes 2048 | tf_op jit(solution)/shard_map/pmax | solution.py:35
  111.2 0.0 copy-start.2
  111.2 8.1 %all-to-all-done = bf16[8,2,64,2048]{3,2,1,0:T(8,128)(2,1)} async-done(((bf16[8,2,64,2048]{3,2,1,0:T(8,128)(2,1)}), bf16[8,2,64,2048]{3,2,1,0:T(8,128)(2,1)}, u32[]{:S(2)}, u32[]{:S(2)}) %all-to-all-start) | async-done | bytes 4194336 | tf_op jit(solution)/shard_map/all_to_all | solution.py:39
  119.3 2.7 %fusion.25 = (bf16[1,8,64,2048]{3,2,0,1:T(8,128)(2,1)S(1)}, bf16[1,8,64,2048]{3,2,0,1:T(8,128)(2,1)S(1)}) fusion(bf16[2,8,64,2048]{3,2,0,1:T(8,128)(2,1)} %bitcast.10), kind=kLoop, calls=%fused_computation.60 | loop fusion | bytes 8388608 | tf_op jit(solution)/shard_map/slice | solution.py:41
  122.1 1.0 fusion.9
  123.1 0.9 fusion.8
  123.9 1.7 convolution_add_fusion.1
  125.6 0.0 reduce-scatter.2.cloned.1.call-update
  125.6 70.6 %reduce-scatter.2.cloned.1.call-done = f32[64,256]{1,0:T(8,128)} async-done(((f32[512,256]{1,0:T(8,128)}), f32[64,256]{1,0:T(8,128)}) %reduce-scatter.2.cloned.1.call-update) | async-done | bytes 65552 | tf_op jit(solution)/shard_map/reduce_scatter | solution.py:42
  196.2 1.6 multiply_reduce_fusion
  197.7 19.3 %psum.7 = f32[256]{0:T(256)S(1)} all-reduce(f32[256]{0:T(256)S(1)} %get-tuple-element.3), channel_id=1, replica_groups=mesh['mp'=8,'rows'=4] {'mp'}, use_global_device_ids=true, to_apply=%region_5.0 | all-reduce | flops 256 | bytes 2048 | tf_op jit(solution)/shard_map/psum | solution.py:44
  217.1 0.0 copy-done.2
  217.1 0.9 fusion.21
  218.0 5.8 %all_gather.3 = f32[64,1024]{1,0:T(8,128)S(1)} all-gather(f32[64,256]{1,0:T(8,128)S(1)} %fusion.21), channel_id=1, replica_groups=mesh['mp'=8,'rows'=4] {'rows'}, dimensions={1}, use_global_device_ids=true | all-gather | bytes 327680 | tf_op jit(solution)/shard_map/all_gather | solution.py:47
  223.8 0.7 copy.13
  (3 shorter events, 0.0 us)
Async XLA Ops:
  7.2 3.5 %copy-start = (f32[64,16384]{1,0:T(8,128)S(1)}, f32[64,16384]{1,0:T(8,128)}, u32[]{:S(2)}) copy-start(f32[64,16384]{1,0:T(8,128)} %param.3) | copy-start | bytes 12582916
  18.5 7.5 %copy-start.1 = (f32[256,2048]{1,0:T(8,128)S(1)}, f32[256,2048]{1,0:T(8,128)}, u32[]{:S(2)}) copy-start(f32[256,2048]{1,0:T(8,128)} %param.2) | copy-start | bytes 6291460
  18.5 100.8 %all-to-all-start = ((bf16[8,2,64,2048]{3,2,1,0:T(8,128)(2,1)}), bf16[8,2,64,2048]{3,2,1,0:T(8,128)(2,1)}, u32[]{:S(2)}, u32[]{:S(2)}) async-start(bf16[8,2,64,2048]{3,2,1,0:T(8,128)(2,1)} %fusion.20), calls=%async_computation | async-start | bytes 8388608 | tf_op jit(solution)/shard_map/all_to_all | solution.py:39
  26.0 170.2 %reduce-scatter.2.cloned.1.call-start = ((), (), s32[]{:S(2)}) async-start(), calls=%async_computation.2 | async-start | bytes 589824 | tf_op jit(solution)/shard_map/reduce_scatter | solution.py:42
  111.2 105.9 %copy-start.2 = (f32[256]{0:T(256)}, f32[256]{0:T(256)S(1)}, u32[]{:S(2)}) copy-start(f32[256]{0:T(256)S(1)} %broadcast_add_fusion) | copy-start | bytes 3076
Sparse Core Ops, SparseCore 0:
  125.7 70.4 reduce-scatter.1
